TPU v7x, 256 devices: a whole 4x4x8 slice. The times are simulated.
256 devices in a mesh: seq: 32 (over y, z), exp: 8 (over x, core).
Axes of the slice: x: 4, y: 4, z: 8, core: 2. Of those that a mesh axis runs over, the one named last changes fastest.
Arguments:
- projected: bfloat16 [3, 4096, 4096], P(None, 'seq', 'exp'), may hold values from -6 to 6
- stream: bfloat16 [4096, 4096], P('seq', 'exp'), may hold values from -6 to 6
- short_filter: float32 [3, 3, 4096], P(None, None, 'exp'), may hold values from -3.5 to 3.5
- long_filter: float32 [4096, 4096], P('seq', 'exp'), may hold values from -0.09375 to 0.09375
- skip_gain: float32 [4096], P('exp'), may hold values from 0.25 to 1.75
- norm_gain: float32 [4096], P('exp'), may hold values from 0.25 to 1.75
- gate_up: bfloat16 [64, 4096, 2, 1408], P('seq', 'exp'), may hold values from -0.125 to 0.125
- down_weight: bfloat16 [64, 1408, 4096], P('seq', None, 'exp'), may hold values from -0.15625 to 0.15625
- expert_ids: int32 [4096, 6], P('seq'), may hold values from 0 to 63, all different within a row; in each aligned block of 128 rows (0 to 127, 128 to 255, ...) at most 16 rows name the same one
- gate_weights: float32 [4096, 6], P('seq'), may hold values from 0.2 to 1
Outputs:
- mixed: bfloat16 [4096, 4096], P('seq', 'exp')
Inputs may be any that keep to these rules, and one draw needn't show every extreme that they name: `expert_ids`: each row names 6 different experts. In each aligned block of 128 rows (the rows of one index of seq) no expert is named more than 16 times, a bound that some block reaches.
All inputs are finite; a program needn't handle non-finite values.
Results may differ from a plain program's by a relative error of at most 0.022.
Values may be sent and summed in bfloat16 or wider, within the bound.
A program may use at most 192 MiB of HBM per device.

v0:
```python
import functools
import math

import jax
import jax.numpy as jnp
from jax import lax
from jax.sharding import PartitionSpec as P

D = 4096


def shifted(value, axis, by):
    devices = lax.axis_size(axis)
    pairs = [(i, i + by) for i in range(devices) if 0 <= i + by < devices]
    return lax.ppermute(value, axis, pairs)


def copy_for_each(value, axis):
    copies = jnp.broadcast_to(value, (lax.axis_size(axis), *value.shape))
    return lax.all_to_all(copies, axis, split_axis=0, concat_axis=0, tiled=True)


def over_copies(value, axis):
    everything = copy_for_each(value, axis)
    return jnp.sum(everything, axis=0)


def angle_table(left_ids, right_ids, modulus):
    product = left_ids[:, None] * right_ids[None, :] % modulus
    return 2.0 * math.pi / modulus * product.astype(jnp.float32)


def precise(formula, matrix, operand):
    return jnp.einsum(formula, matrix, operand, precision=lax.Precision.HIGHEST)


def local_long(whole, slab_count, tok_rows):
    blocks = 2 * slab_count
    points = blocks * tok_rows
    width = whole.shape[2]
    arranged = whole.reshape(2, slab_count, tok_rows, width)
    slab_ids = jnp.arange(slab_count, dtype=jnp.int32)
    frequency_index = jnp.arange(blocks, dtype=jnp.int32)
    row_ids = jnp.arange(tok_rows, dtype=jnp.int32)
    outer_angle = angle_table(frequency_index, slab_ids, blocks)
    first_re = precise("kp,apmc->akmc", jnp.cos(outer_angle), arranged)
    first_im = -precise("kp,apmc->akmc", jnp.sin(outer_angle), arranged)
    twiddle = angle_table(frequency_index, row_ids, points)
    turn_cos = jnp.cos(twiddle)[None, :, :, None]
    turn_sin = jnp.sin(twiddle)[None, :, :, None]
    turned_re = first_re * turn_cos + first_im * turn_sin
    turned_im = first_im * turn_cos - first_re * turn_sin
    inner_rotation = angle_table(row_ids, row_ids, tok_rows)
    inner_cos = jnp.cos(inner_rotation)
    inner_sin = jnp.sin(inner_rotation)
    spec_re = precise("qm,akmc->akqc", inner_cos, turned_re) + precise(
        "qm,akmc->akqc", inner_sin, turned_im
    )
    spec_im = precise("qm,akmc->akqc", inner_cos, turned_im) - precise(
        "qm,akmc->akqc", inner_sin, turned_re
    )
    joint_re = spec_re[0] * spec_re[1] - spec_im[0] * spec_im[1]
    joint_im = spec_re[0] * spec_im[1] + spec_im[0] * spec_re[1]
    back_re = precise("mq,kqc->kmc", inner_cos, joint_re) - precise(
        "mq,kqc->kmc", inner_sin, joint_im
    )
    back_im = precise("mq,kqc->kmc", inner_cos, joint_im) + precise(
        "mq,kqc->kmc", inner_sin, joint_re
    )
    back_cos = jnp.cos(twiddle)[:, :, None]
    back_sin = jnp.sin(twiddle)[:, :, None]
    reverted_re = back_re * back_cos - back_im * back_sin
    reverted_im = back_re * back_sin + back_im * back_cos
    last_angle = angle_table(slab_ids, frequency_index, blocks)
    inverted = (
        precise("pk,kmc->pmc", jnp.cos(last_angle), reverted_re)
        - precise("pk,kmc->pmc", jnp.sin(last_angle), reverted_im)
    ) / points
    return inverted.reshape(slab_count * tok_rows, width)


def expert_work(received, gate_up, down_weight):
    partials = jnp.einsum("spnc,pcgf->spngf", received, gate_up, preferred_element_type=jnp.float32)
    totals = lax.psum(partials.astype(jnp.bfloat16), "exp").astype(jnp.float32)
    hidden_state = (jax.nn.silu(totals[:, :, :, 0]) * totals[:, :, :, 1]).astype(jnp.bfloat16)
    final_output = jnp.einsum(
        "hgtq,gqr->hgtr", hidden_state, down_weight, preferred_element_type=jnp.float32
    )
    outgoing = final_output.astype(jnp.bfloat16)
    return lax.all_to_all(outgoing, "seq", split_axis=0, concat_axis=0, tiled=True)


def local(
    projected,
    stream,
    short_filter,
    long_filter,
    skip_gain,
    norm_gain,
    gate_up,
    down_weight,
    expert_ids,
    gate_weights,
):
    seq_count = lax.axis_size("seq")
    tok_rows = projected.shape[1]
    channels = projected.shape[2]
    tap_count = short_filter.shape[1]
    earlier = shifted(projected[:, tok_rows - (tap_count - 1) :, :], "seq", 1)
    extended = jnp.concatenate([earlier, projected], axis=1).astype(jnp.float32)
    mixed_short = short_filter[:, 0][:, None, :] * extended[:, tap_count - 1 :]
    for offset in range(1, tap_count):
        begin = tap_count - 1 - offset
        mixed_short = (
            mixed_short
            + short_filter[:, offset][:, None, :] * extended[:, begin : begin + tok_rows]
        )
    queries = mixed_short[0]
    key_side = mixed_short[1]
    valued = mixed_short[2]
    product = key_side * valued
    paired = jnp.stack([product, long_filter])
    whole = lax.all_to_all(
        paired.astype(jnp.bfloat16), "seq", split_axis=2, concat_axis=1, tiled=True
    ).astype(paired.dtype)
    result_long = local_long(whole, seq_count, tok_rows)
    convolved = lax.all_to_all(
        result_long.astype(jnp.bfloat16), "seq", split_axis=0, concat_axis=1, tiled=True
    ).astype(result_long.dtype)
    mixed_long = queries * (convolved + skip_gain * product)
    residual = (stream.astype(jnp.float32) + mixed_long).astype(jnp.bfloat16)
    resid_float = residual.astype(jnp.float32)
    squared_values = over_copies(jnp.sum(resid_float * resid_float, axis=1), "exp")
    root_mean = jnp.sqrt(squared_values / D + 1e-06)
    normed = (resid_float / root_mean[:, None] * norm_gain).astype(jnp.bfloat16)
    top_count = expert_ids.shape[1]
    local_experts = gate_up.shape[0]
    experts = local_experts * seq_count
    capacity = tok_rows * top_count * 4 // (experts * 3)
    flat_ids = expert_ids.reshape(-1)
    onehot = (flat_ids[:, None] == jnp.arange(experts, dtype=jnp.int32)[None, :]).astype(jnp.int32)
    before = jnp.cumsum(onehot, axis=0) - onehot
    slot_ids = jnp.sum(before * onehot, axis=1)
    target = flat_ids * capacity + slot_ids
    token_rows = jnp.arange(tok_rows * top_count, dtype=jnp.int32) // top_count + 1
    sources = jnp.zeros((experts * capacity,), jnp.int32).at[target].set(token_rows)
    padded = jnp.concatenate([jnp.zeros((1, channels), jnp.bfloat16), normed], axis=0)
    outgoing = padded[sources].reshape(seq_count, local_experts, capacity, channels)
    worker = functools.partial(expert_work, gate_up=gate_up, down_weight=down_weight)
    returned = worker(lax.all_to_all(outgoing, "seq", split_axis=0, concat_axis=0, tiled=True))
    flat_back = returned.reshape(experts * capacity, channels)
    picked = flat_back[target].reshape(tok_rows, top_count, channels).astype(jnp.float32)
    combined = jnp.zeros((tok_rows, channels), jnp.float32)
    for pick_k in range(top_count):
        combined = combined + gate_weights[:, pick_k : pick_k + 1] * picked[:, pick_k]
    return (resid_float + combined).astype(jnp.bfloat16)


def solution(mesh):
    in_specs = (
        P(None, "seq", "exp"),
        P("seq", "exp"),
        P(None, None, "exp"),
        P("seq", "exp"),
        P("exp"),
        P("exp"),
        P("seq", "exp", None, None),
        P("seq", None, "exp"),
        P("seq", None),
        P("seq", None),
    )
    out_specs = P("seq", "exp")
    return jax.shard_map(local, mesh=mesh, in_specs=in_specs, out_specs=out_specs, check_vma=False)
```

profile of v0, /device:TPU:5, one launch (start us, length us, event | category | flops | bytes accessed | tf_op | source)
XLA Modules:
  0.0 272.3 jit_solution(5783752731659330634)
XLA Ops:
  6.5 0.9 slice.95
  7.5 3.5 %collective-permute-start = (bf16[3,2,512]{2,1,0:T(2,128)(2,1)S(1)}, bf16[3,2,512]{2,1,0:T(2,128)(2,1)S(1)}, u32[]{:S(2)}, u32[]{:S(2)}) collective-permute-start(bf16[3,2,512]{2,1,0:T(2,128)(2,1)S(1)} %slice.95), channel_id=1, source_target_pairs={{0,8},{8,16},{16,24},{24,32},{32,40},{40,48},{48,56},{56,64},{64,7... | collective-permute-start | bytes 18440 | tf_op jit(solution)/shard_map/ppermute | solution.py:15
  11.0 0.9 fusion.185
  11.9 1.0 convert_bitcast_fusion.1
  12.9 0.8 copy.106
  13.8 1.1 maximum_convert_fusion
  14.9 0.2 fusion.31
  15.2 0.9 copy-done.1
  16.2 0.9 copy.93
  17.0 10.4 %all-to-all-start = ((bf16[2,128,512]{1,0,2:T(2,128)(2,1)}), bf16[2,128,512]{1,0,2:T(2,128)(2,1)S(1)}, u32[]{:S(2)}, u32[]{:S(2)}) async-start(bf16[2,128,512]{1,0,2:T(2,128)(2,1)} %copy.93), calls=%async_computation | async-start | bytes 524288 | tf_op jit(solution)/shard_map/all_to_all | solution.py:123
  27.5 1.8 reduce-window.6
  29.3 0.1 fusion.112
  29.4 0.3 slice_reduce_fusion
  29.7 7.4 %all-to-all-done = bf16[2,128,512]{1,0,2:T(2,128)(2,1)S(1)} async-done(((bf16[2,128,512]{1,0,2:T(2,128)(2,1)}), bf16[2,128,512]{1,0,2:T(2,128)(2,1)S(1)}, u32[]{:S(2)}, u32[]{:S(2)}) %all-to-all-start) | async-done | bytes 262176 | tf_op jit(solution)/shard_map/all_to_all | solution.py:123
  37.1 0.7 convolution_bitcast_fusion
  37.8 0.9 multiply_add_fusion
  38.7 1.7 fusion.29
  40.5 1.7 fusion.25
  42.2 1.7 fusion.20
  43.9 1.7 fusion.19
  45.8 0.8 fusion.33
  46.6 0.8 fusion.37
  47.5 0.8 convolution_add_fusion.1
  48.3 1.1 add_bitcast_fusion
  49.4 0.6 fusion.40
  49.9 0.6 fusion.23
  50.5 0.7 copy.102
  51.2 5.2 %all-to-all-start.1 = ((bf16[32,128,16]{1,2,0:T(8,128)(2,1)}), bf16[32,128,16]{1,2,0:T(8,128)(2,1)S(1)}, u32[]{:S(2)}, u32[]{:S(2)}) async-start(bf16[32,128,16]{1,2,0:T(8,128)(2,1)} %copy.102), calls=%async_computation.1 | async-start | bytes 262144 | tf_op jit(solution)/shard_map/all_to_all | solution.py:127
  56.7 0.1 mul.518
  57.0 3.4 %scatter_custom_fusion = s32[1024]{0:T(1024)S(1)} fusion(s32[768]{0:T(1024)S(1)} %fusion.131, s32[768]{0:T(1024)S(1)} %fusion.126, s32[]{:T(128)} %constant.77.clone.1), kind=kCustom, calls=%fused_computation.174 | custom fusion | bytes 4100 | tf_op jit(solution)/shard_map/scatter | solution.py:146
  60.4 5.2 %all-to-all-done.1 = bf16[32,128,16]{1,2,0:T(8,128)(2,1)S(1)} async-done(((bf16[32,128,16]{1,2,0:T(8,128)(2,1)}), bf16[32,128,16]{1,2,0:T(8,128)(2,1)S(1)}, u32[]{:S(2)}, u32[]{:S(2)}) %all-to-all-start.1) | async-done | bytes 131104 | tf_op jit(solution)/shard_map/all_to_all | solution.py:127
  65.7 1.3 fusion.42
  67.1 0.6 broadcast_in_dim.4
  67.7 8.6 %all-to-all-start.2 = ((f32[8,1,128]{2,1,0:T(1,128)}), f32[8,1,128]{2,1,0:T(1,128)S(1)}, u32[]{:S(2)}, u32[]{:S(2)}) async-start(f32[8,1,128]{2,1,0:T(1,128)} %broadcast_in_dim.4), calls=%async_computation.2 | async-start | bytes 8192 | tf_op jit(solution)/shard_map/all_to_all | solution.py:20
  76.2 2.5 all-to-all-done.2
  79.0 5.1 %gather_fusion = bf16[1024,512]{1,0:T(8,128)(2,1)} fusion(bf16[129,512]{1,0:T(8,128)(2,1)S(1)} %concatenate.7, s32[1024]{0:T(1024)S(1)} %fusion.129), kind=kCustom, calls=%fused_computation | custom fusion | bytes 2101248 | tf_op jit(solution)/shard_map/gather | solution.py:148
  84.0 29.1 %all_to_all.41 = bf16[32,2,16,512]{3,2,1,0:T(8,128)(2,1)S(1)} all-to-all(bf16[32,2,16,512]{3,2,1,0:T(8,128)(2,1)} %bitcast.225), channel_id=1, replica_groups=mesh['seq'=32,'exp'=8] {'seq'}, dimensions={0} | all-to-all | bytes 2097152 | tf_op jit(solution)/shard_map/all_to_all | solution.py:150
  113.2 7.6 %convert_bitcast_fusion = bf16[32,2,16,2,1408]{4,2,3,0,1:T(8,128)(2,1)} fusion(bf16[2,512,2,1408,1]{3,2,1,0,4:T(2,128)(2,1)} %bitcast.232, bf16[32,2,16,512]{3,2,1,0:T(8,128)(2,1)S(1)} %all_to_all.41), kind=kOutput, calls=%fused_computation.9 | convolution fusion | flops 2955673600 | bytes 12582912 | tf_op jit(solution)/shard_map/spnc,pcgf->spngf/dot_general | solution.py:83
  120.8 84.8 %all-reduce.3.cloned.1.call-done = bf16[32,2,16,2,1408]{4,2,3,0,1:T(8,128)(2,1)} async-done(((bf16[32,2,16,2,1408]{4,2,3,0,1:T(8,128)(2,1)}), bf16[32,2,16,2,1408]{4,2,3,0,1:T(8,128)(2,1)}) %all-reduce.3.cloned.1.call-update) | async-done | bytes 5767184 | tf_op jit(solution)/shard_map/psum | solution.py:84
  205.6 4.2 %convert_element_type.139 = f32[32,2,16,2,1408]{4,2,3,0,1:T(8,128)S(1)} convert(bf16[32,2,16,2,1408]{4,2,3,0,1:T(8,128)(2,1)} %all-reduce.3.cloned.1.call-done) | non-fusion elementwise | flops 2883584 | bytes 17301504 | tf_op jit(solution)/shard_map/convert_element_type | solution.py:84
  209.8 2.1 fusion.14
  212.0 1.1 copy.112
  213.1 9.7 %all-to-all-start.4 = ((bf16[32,2,16,512]{3,2,1,0:T(8,128)(2,1)}), bf16[32,2,16,512]{3,2,1,0:T(8,128)(2,1)}, u32[]{:S(2)}, u32[]{:S(2)}) async-start(bf16[32,2,16,512]{3,2,1,0:T(8,128)(2,1)} %copy.112), calls=%async_computation.4 | async-start | bytes 2097152 | tf_op jit(solution)/shard_map/all_to_all | solution.py:90
  222.8 27.7 %all-to-all-done.4 = bf16[32,2,16,512]{3,2,1,0:T(8,128)(2,1)} async-done(((bf16[32,2,16,512]{3,2,1,0:T(8,128)(2,1)}), bf16[32,2,16,512]{3,2,1,0:T(8,128)(2,1)}, u32[]{:S(2)}, u32[]{:S(2)}) %all-to-all-start.4) | async-done | bytes 1048608 | tf_op jit(solution)/shard_map/all_to_all | solution.py:90
  250.5 4.7 %gather_fusion.1 = bf16[768,512]{1,0:T(8,128)(2,1)} fusion(bf16[1024,512]{1,0:T(8,128)(2,1)} %bitcast.41, s32[1024]{0:T(1024)S(1)} %pad_clamp_fusion), kind=kCustom, calls=%fused_computation.1 | custom fusion | bytes 1575936 | tf_op jit(solution)/shard_map/gather | solution.py:152
  255.2 2.5 reshape.159
  257.7 6.9 %fusion.184 = (f32[128,1,512]{2,1,0:T(1,128)S(1)}, f32[128,1,512]{2,1,0:T(1,128)S(1)}, f32[128,1,512]{2,1,0:T(1,128)S(1)}, f32[128,1,512]{2,1,0:T(1,128)S(1)}, f...) fusion(f32[128,6,512]{2,1,0:T(8,128)} %reshape.159), kind=kLoop, calls=%fused_computation.232 | loop fusion | bytes 3145728 | tf_op jit(solution)/shard_map/slice | solution.py:155
  264.6 0.8 fusion.45
  (41 shorter events, 1.2 us)
Async XLA Ops:
  6.5 203.3 %copy-start = (bf16[2,1408,512]{2,1,0:T(8,128)(2,1)S(1)}, bf16[2,1408,512]{2,1,0:T(8,128)(2,1)}, u32[]{:S(2)}) copy-start(bf16[2,1408,512]{2,1,0:T(8,128)(2,1)} %param.17) | copy-start | bytes 8650756
  6.5 23.2 %copy-start.4 = (s32[128,6]{0,1:T(8,128)S(1)}, s32[128,6]{0,1:T(8,128)}, u32[]{:S(2)}) copy-start(s32[128,6]{0,1:T(8,128)} %param.18) | copy-start | bytes 9220
  7.5 6.4 %collective-permute-start = (bf16[3,2,512]{2,1,0:T(2,128)(2,1)S(1)}, bf16[3,2,512]{2,1,0:T(2,128)(2,1)S(1)}, u32[]{:S(2)}, u32[]{:S(2)}) collective-permute-start(bf16[3,2,512]{2,1,0:T(2,128)(2,1)S(1)} %slice.95), channel_id=1, source_target_pairs={{0,8},{8,16},{16,24},{24,32},{32,40},{40,48},{48,56},{56,64},{64,7... | collective-permute-start | bytes 18440 | tf_op jit(solution)/shard_map/ppermute | solution.py:15
  13.7 1.5 copy-start.2
  15.2 0.9 copy-start.1
  17.0 20.1 %all-to-all-start = ((bf16[2,128,512]{1,0,2:T(2,128)(2,1)}), bf16[2,128,512]{1,0,2:T(2,128)(2,1)S(1)}, u32[]{:S(2)}, u32[]{:S(2)}) async-start(bf16[2,128,512]{1,0,2:T(2,128)(2,1)} %copy.93), calls=%async_computation | async-start | bytes 524288 | tf_op jit(solution)/shard_map/all_to_all | solution.py:123
  45.6 10.8 %copy-start.3 = (s32[128,6]{1,0:T(8,128)S(1)}, s32[128,6]{1,0:T(8,128)}, u32[]{:S(2)}) copy-start(s32[128,6]{1,0:T(8,128)} %copy-done.2) | copy-start | bytes 9220
  45.7 20.1 %copy-start.6 = (f32[512]{0:T(512)S(1)}, f32[512]{0:T(512)}, u32[]{:S(2)}) copy-start(f32[512]{0:T(512)} %param.14) | copy-start | bytes 6148
  45.8 33.0 %copy-start.7 = (f32[512]{0:T(512)S(1)}, f32[512]{0:T(512)}, u32[]{:S(2)}) copy-start(f32[512]{0:T(512)} %param.15) | copy-start | bytes 6148
  51.2 14.4 %all-to-all-start.1 = ((bf16[32,128,16]{1,2,0:T(8,128)(2,1)}), bf16[32,128,16]{1,2,0:T(8,128)(2,1)S(1)}, u32[]{:S(2)}, u32[]{:S(2)}) async-start(bf16[32,128,16]{1,2,0:T(8,128)(2,1)} %copy.102), calls=%async_computation.1 | async-start | bytes 262144 | tf_op jit(solution)/shard_map/all_to_all | solution.py:127
  67.7 11.1 %all-to-all-start.2 = ((f32[8,1,128]{2,1,0:T(1,128)}), f32[8,1,128]{2,1,0:T(1,128)S(1)}, u32[]{:S(2)}, u32[]{:S(2)}) async-start(f32[8,1,128]{2,1,0:T(1,128)} %broadcast_in_dim.4), calls=%async_computation.2 | async-start | bytes 8192 | tf_op jit(solution)/shard_map/all_to_all | solution.py:20
  76.2 129.4 %all-reduce.3.cloned.1.call-start = ((), (), s32[]{:S(2)}) async-start(), calls=%async_computation.5 | async-start | bytes 11534336 | tf_op jit(solution)/shard_map/psum | solution.py:84
  209.8 13.0 %copy-start.5 = (f32[128,6]{0,1:T(8,128)S(1)}, f32[128,6]{0,1:T(8,128)}, u32[]{:S(2)}) copy-start(f32[128,6]{0,1:T(8,128)} %param.19) | copy-start | bytes 9220
  213.1 37.5 %all-to-all-start.4 = ((bf16[32,2,16,512]{3,2,1,0:T(8,128)(2,1)}), bf16[32,2,16,512]{3,2,1,0:T(8,128)(2,1)}, u32[]{:S(2)}, u32[]{:S(2)}) async-start(bf16[32,2,16,512]{3,2,1,0:T(8,128)(2,1)} %copy.112), calls=%async_computation.4 | async-start | bytes 2097152 | tf_op jit(solution)/shard_map/all_to_all | solution.py:90
Sparse Core Ops, SparseCore 0:
  120.9 84.6 all-reduce.2
where the time goes:
time: 275 us; the launch traced here: 272 us
  waiting for transfers between devices  128 us (47%)
  starting transfers between devices  37.4 us (14%)
  local copies, waits for them, and re-layouts  30.2 us (11%)
  blocking collectives  29.1 us (11%)
  matrix products  22.9 us (8%)
  between operations  13.8 us (5%)
  other arithmetic  11.2 us (4%)
    psum x1, waiting for transfers between devices, expert_work(): totals = lax.psum(partials.astype(jnp.bfloat16), 'exp').astype(jnp.float32)  84.8 us
    all_to_all x1, blocking collectives, local(): lax.all_to_all(outgoing, 'seq', split_axis=0, concat_axis=0, tiled=True)  29.1 us
    all_to_all x1, waiting for transfers between devices, expert_work(): lax.all_to_all(outgoing, 'seq', split_axis=0, concat_axis=0, tiled=True)  27.7 us
    dot_general x12, matrix products, precise(): return jnp.einsum(formula, matrix, operand, precision=lax.Precision.HIGHEST)  13.1 us
    all_to_all x1, starting transfers between devices, local(): lax.all_to_all(paired.astype(jnp.bfloat16), 'seq', split_axis=2, concat_a...  10.4 us
    all_to_all x1, starting transfers between devices, expert_work(): lax.all_to_all(outgoing, 'seq', split_axis=0, concat_axis=0, tiled=True)  9.7 us
    all_to_all x1, starting transfers between devices, copy_for_each(): return lax.all_to_all(copies, axis, split_axis=0, concat_axis=0, tiled=True)  8.56 us
    dot_general x1, matrix products, expert_work(): jnp.einsum('spnc,pcgf->spngf', received, gate_up, preferred_element_type=...  7.6 us
  transfers between devices with their start and end apart: 6, of which 5 were waited for; matrix products, arithmetic and copies ran while one was open for 3% of the time, Pallas kernels for 0%

commit v1 on v0

--- a/solution.py
+++ b/solution.py
@@ -1,9 +1,10 @@
-import functools
 import math
 
 import jax
 import jax.numpy as jnp
 from jax import lax
+from jax.experimental import pallas as pl
+from jax.experimental.pallas import tpu as pltpu
 from jax.sharding import PartitionSpec as P
 
 D = 4096
@@ -79,15 +80,344 @@
     return inverted.reshape(slab_count * tok_rows, width)
 
 
-def expert_work(received, gate_up, down_weight):
-    partials = jnp.einsum("spnc,pcgf->spngf", received, gate_up, preferred_element_type=jnp.float32)
-    totals = lax.psum(partials.astype(jnp.bfloat16), "exp").astype(jnp.float32)
-    hidden_state = (jax.nn.silu(totals[:, :, :, 0]) * totals[:, :, :, 1]).astype(jnp.bfloat16)
-    final_output = jnp.einsum(
-        "hgtq,gqr->hgtr", hidden_state, down_weight, preferred_element_type=jnp.float32
-    )
-    outgoing = final_output.astype(jnp.bfloat16)
-    return lax.all_to_all(outgoing, "seq", split_axis=0, concat_axis=0, tiled=True)
+MESH = pl.DeviceIdType.MESH
+SLOTS = 16
+HALF = 512
+HIDDEN = 1408
+
+
+def dot(left, right):
+    return jnp.dot(left, right, preferred_element_type=jnp.float32)
+
+
+def remote(src, dst, send, recv, seq, exp):
+    return pltpu.make_async_remote_copy(
+        src_ref=src,
+        dst_ref=dst,
+        send_sem=send,
+        recv_sem=recv,
+        device_id=(seq, exp),
+        device_id_type=MESH,
+    )
+
+
+def rows(start, size):
+    return pl.ds(pl.multiple_of(start, size), size)
+
+
+def experts_kernel(
+    normed,
+    resid,
+    ids,
+    weights,
+    gate_up,
+    down,
+    out,
+    packed,
+    recv,
+    wg,
+    wd,
+    far_out,
+    far_in,
+    near_out,
+    near_in,
+    held,
+    hidden,
+    outgoing,
+    returned,
+    chosen_hi,
+    chosen_lo,
+    local_sem,
+    swap_send,
+    swap_recv,
+    out_send,
+    out_recv,
+    far_send,
+    far_recv,
+    near_send,
+    near_recv,
+    hid_send,
+    hid_recv,
+    fwd_send,
+    fwd_recv,
+    back_send,
+    back_recv,
+):
+    seq = lax.axis_index("seq")
+    exp = lax.axis_index("exp")
+    core = lax.rem(exp, 2)
+    chip = exp // 2
+    column = 2 * chip
+    partner = column + 1 - core
+    after = lax.rem(chip + 1, 4)
+    before = lax.rem(chip + 3, 4)
+    across = lax.rem(chip + 2, 4)
+    exp_after = 2 * after + core
+    exp_before = 2 * before + core
+
+    own_gate = pltpu.make_async_copy(gate_up.at[core], wg.at[core], local_sem.at[0])
+    own_down = pltpu.make_async_copy(down.at[core], wd.at[core], local_sem.at[1])
+    own_gate.start()
+    own_down.start()
+
+    barrier = pltpu.get_barrier_semaphore()
+
+    def greet(i, carry):
+        other = lax.rem(seq + i, 32)
+        for side in range(2):
+            pl.semaphore_signal(barrier, inc=1, device_id=(other, column + side), device_id_type=MESH)
+        return carry
+
+    lax.fori_loop(1, 32, greet, 0)
+    for other in (partner, exp_after, exp_before):
+        pl.semaphore_signal(barrier, inc=1, device_id=(seq, other), device_id_type=MESH)
+
+    tokens = ids.shape[0]
+    lanes = lax.broadcasted_iota(jnp.int32, (tokens, 128), 1)
+    named = jnp.zeros((tokens, 128), jnp.float32)
+    scale = jnp.zeros((tokens, 128), jnp.float32)
+    for k in range(ids.shape[1]):
+        hit = ids[:, k : k + 1] == lanes
+        named = jnp.where(hit, 1.0, named)
+        scale = jnp.where(hit, weights[:, k : k + 1], scale)
+    row_ids = lax.broadcasted_iota(jnp.int32, (tokens, tokens), 0)
+    col_ids = lax.broadcasted_iota(jnp.int32, (tokens, tokens), 1)
+    earlier = jnp.where(col_ids < row_ids, 1.0, 0.0).astype(jnp.bfloat16)
+    rank = dot(earlier, named.astype(jnp.bfloat16))
+    number = named * (rank + 1.0)
+    slot_rows = 64 * SLOTS
+    spread_row = lax.broadcasted_iota(jnp.int32, (slot_rows, 128), 0)
+    spread_col = lax.broadcasted_iota(jnp.int32, (slot_rows, 128), 1)
+    spread = jnp.where(spread_row // SLOTS == spread_col, 1.0, 0.0).astype(jnp.bfloat16)
+    number_rows = dot(spread, number.T.astype(jnp.bfloat16))
+    wanted = (lax.rem(spread_row, SLOTS) + 1).astype(jnp.float32)
+    pick = jnp.where(number_rows == wanted, 1.0, 0.0).astype(jnp.bfloat16)
+    packed[...] = dot(pick, normed[...]).astype(jnp.bfloat16)
+
+    own_row = (core * 32 + seq) * SLOTS
+    pl.semaphore_wait(barrier, 65)
+
+    swap_gate = remote(gate_up.at[1 - core], wg.at[core], swap_send.at[0], swap_recv.at[0], seq, partner)
+    swap_down = remote(down.at[1 - core], wd.at[core], swap_send.at[1], swap_recv.at[1], seq, partner)
+    swap_gate.start()
+
+    def send_rows(other, side):
+        remote(
+            packed.at[rows((2 * other + side) * SLOTS, SLOTS)],
+            recv.at[rows(own_row, SLOTS)],
+            out_send,
+            out_recv,
+            other,
+            column + side,
+        ).start()
+
+    def dispatch(i, carry):
+        other = lax.rem(seq + i, 32)
+        for side in range(2):
+            send_rows(other, side)
+        return carry
+
+    lax.fori_loop(1, 32, dispatch, 0)
+    send_rows(seq, 1 - core)
+    swap_down.start()
+    recv[rows(own_row, SLOTS)] = packed[rows((2 * seq + core) * SLOTS, SLOTS)]
+
+    turn_row = lax.broadcasted_iota(jnp.int32, (128, slot_rows), 0)
+    turn_col = lax.broadcasted_iota(jnp.int32, (128, slot_rows), 1)
+    turned = jnp.where(turn_col // SLOTS == turn_row, 1.0, 0.0).astype(jnp.bfloat16)
+    number_cols = dot(number.astype(jnp.bfloat16), turned)
+    matched = number_cols == (lax.rem(turn_col, SLOTS) + 1).astype(jnp.float32)
+    scale_hi = scale.astype(jnp.bfloat16)
+    scale_lo = (scale - scale_hi.astype(jnp.float32)).astype(jnp.bfloat16)
+    chosen_hi[...] = jnp.where(matched, dot(scale_hi, turned), 0.0).astype(jnp.bfloat16)
+    chosen_lo[...] = jnp.where(matched, dot(scale_lo, turned), 0.0).astype(jnp.bfloat16)
+
+    own_gate.wait()
+    swap_gate.wait()
+    received = pl.ds(0, 63 * SLOTS)
+    remote(packed.at[received], recv.at[received], out_send, out_recv, seq, partner).wait()
+
+    def partial(quarter, which):
+        first = recv[rows(quarter * 128, 128)]
+        second = recv[rows(HALF + quarter * 128, 128)]
+        return dot(first, wg[0, which]) + dot(second, wg[1, which])
+
+    far_gate = remote(far_out.at[0], far_in.at[0], far_send.at[0], far_recv.at[0], seq, exp_after)
+    far_up = remote(far_out.at[1], far_in.at[1], far_send.at[1], far_recv.at[1], seq, exp_before)
+    far_out[0] = partial(across, 0).astype(jnp.bfloat16)
+    far_gate.start()
+    far_out[1] = partial(across, 1).astype(jnp.bfloat16)
+    far_up.start()
+
+    def near(direction, which):
+        return remote(
+            near_out.at[direction, which],
+            near_in.at[direction, which],
+            near_send.at[direction, which],
+            near_recv.at[direction, which],
+            seq,
+            (exp_after, exp_before)[direction],
+        )
+
+    near_out[0, 1] = partial(after, 1).astype(jnp.bfloat16)
+    near(0, 1).start()
+    near_out[1, 0] = partial(before, 0).astype(jnp.bfloat16)
+    near(1, 0).start()
+    held[0] = partial(after, 0)
+    held[1] = partial(before, 1)
+    far_gate.wait_recv()
+    near_out[0, 0] = (held[0] + far_in[0].astype(jnp.float32)).astype(jnp.bfloat16)
+    near(0, 0).start()
+    far_up.wait_recv()
+    near_out[1, 1] = (held[1] + far_in[1].astype(jnp.float32)).astype(jnp.bfloat16)
+    near(1, 1).start()
+    held[0] = partial(chip, 0)
+    held[1] = partial(chip, 1)
+    near(0, 1).wait_recv()
+    near(1, 0).wait_recv()
+    near(0, 0).wait_recv()
+    near(1, 1).wait_recv()
+
+    gate = held[0] + near_in[0, 0].astype(jnp.float32) + near_in[1, 0].astype(jnp.float32)
+    up = held[1] + near_in[0, 1].astype(jnp.float32) + near_in[1, 1].astype(jnp.float32)
+    hidden[chip] = (gate / (1.0 + jnp.exp(-gate)) * up).astype(jnp.bfloat16)
+
+    def share(direction):
+        return remote(
+            hidden.at[chip],
+            hidden.at[chip],
+            hid_send.at[direction],
+            hid_recv.at[direction],
+            seq,
+            (exp_after, exp_before)[direction],
+        )
+
+    def arrived(direction):
+        quarter = (before, after)[direction]
+        return remote(
+            hidden.at[quarter],
+            hidden.at[quarter],
+            hid_send.at[direction],
+            hid_recv.at[direction],
+            seq,
+            (exp_after, exp_before)[direction],
+        )
+
+    def forward(direction, quarter):
+        part = pl.ds(64 * direction, 64)
+        return remote(
+            hidden.at[quarter, part],
+            hidden.at[quarter, part],
+            fwd_send.at[direction],
+            fwd_recv.at[direction],
+            seq,
+            (exp_after, exp_before)[direction],
+        )
+
+    share(0).start()
+    share(1).start()
+    own_down.wait()
+    swap_down.wait()
+
+    back_row = (2 * seq + core) * SLOTS
+
+    def give_back(quarter):
+        values = hidden[quarter]
+        for side in range(2):
+            outgoing[side, rows(quarter * 128, 128)] = dot(values, wd[side]).astype(jnp.bfloat16)
+
+        def send_back(i, carry):
+            other = quarter * 8 + lax.rem(seq + i, 8)
+            for side in range(2):
+
+                @pl.when(jnp.logical_or(other != seq, side != core))
+                def _():
+                    remote(
+                        outgoing.at[side, rows(other * SLOTS, SLOTS)],
+                        returned.at[rows(back_row, SLOTS)],
+                        back_send,
+                        back_recv,
+                        other,
+                        column + side,
+                    ).start()
+
+            return carry
+
+        lax.fori_loop(0, 8, send_back, 0)
+
+    give_back(chip)
+    arrived(0).wait_recv()
+    forward(0, before).start()
+    arrived(1).wait_recv()
+    forward(1, after).start()
+    give_back(before)
+    give_back(after)
+    forward(0, across).wait_recv()
+    forward(1, across).wait_recv()
+    give_back(across)
+    returned[rows(back_row, SLOTS)] = outgoing[core, rows(seq * SLOTS, SLOTS)]
+
+    far_gate.wait_send()
+    far_up.wait_send()
+    for direction in range(2):
+        for which in range(2):
+            near(direction, which).wait_send()
+        share(direction).wait_send()
+    forward(0, before).wait_send()
+    forward(1, after).wait_send()
+
+    remote(packed.at[received], returned.at[received], back_send, back_recv, seq, partner).wait()
+    combined = dot(chosen_hi[...], returned[...]) + dot(chosen_lo[...], returned[...])
+    out[...] = (resid[...].astype(jnp.float32) + combined).astype(jnp.bfloat16)
+
+
+def experts(normed, resid, ids, weights, gate_up, down):
+    tokens, width = normed.shape
+    vmem = pl.BlockSpec(memory_space=pltpu.VMEM)
+    anywhere = pl.BlockSpec(memory_space=pl.ANY)
+    bf16, f32 = jnp.bfloat16, jnp.float32
+    dma = pltpu.SemaphoreType.DMA
+    return pl.pallas_call(
+        experts_kernel,
+        out_shape=jax.ShapeDtypeStruct((tokens, width), bf16),
+        in_specs=[vmem, vmem, vmem, vmem, anywhere, anywhere],
+        out_specs=vmem,
+        scratch_shapes=[
+            pltpu.VMEM((64 * SLOTS, width), bf16),
+            pltpu.VMEM((64 * SLOTS, width), bf16),
+            pltpu.VMEM((2, 2, width, HIDDEN), bf16),
+            pltpu.VMEM((2, HIDDEN, width), bf16),
+            pltpu.VMEM((2, 128, HIDDEN), bf16),
+            pltpu.VMEM((2, 128, HIDDEN), bf16),
+            pltpu.VMEM((2, 2, 128, HIDDEN), bf16),
+            pltpu.VMEM((2, 2, 128, HIDDEN), bf16),
+            pltpu.VMEM((2, 128, HIDDEN), f32),
+            pltpu.VMEM((4, 128, HIDDEN), bf16),
+            pltpu.VMEM((2, HALF, width), bf16),
+            pltpu.VMEM((64 * SLOTS, width), bf16),
+            pltpu.VMEM((tokens, 64 * SLOTS), bf16),
+            pltpu.VMEM((tokens, 64 * SLOTS), bf16),
+            dma((2,)),
+            dma((2,)),
+            dma((2,)),
+            dma,
+            dma,
+            dma((2,)),
+            dma((2,)),
+            dma((2, 2)),
+            dma((2, 2)),
+            dma((2,)),
+            dma((2,)),
+            dma((2,)),
+            dma((2,)),
+            dma,
+            dma,
+        ],
+        compiler_params=pltpu.CompilerParams(
+            collective_id=0, has_side_effects=True, vmem_limit_bytes=48 * 1024 * 1024
+        ),
+        name="experts",
+    )(normed, resid, ids, weights, gate_up, down)
 
 
 def local(
@@ -133,27 +463,8 @@
     squared_values = over_copies(jnp.sum(resid_float * resid_float, axis=1), "exp")
     root_mean = jnp.sqrt(squared_values / D + 1e-06)
     normed = (resid_float / root_mean[:, None] * norm_gain).astype(jnp.bfloat16)
-    top_count = expert_ids.shape[1]
-    local_experts = gate_up.shape[0]
-    experts = local_experts * seq_count
-    capacity = tok_rows * top_count * 4 // (experts * 3)
-    flat_ids = expert_ids.reshape(-1)
-    onehot = (flat_ids[:, None] == jnp.arange(experts, dtype=jnp.int32)[None, :]).astype(jnp.int32)
-    before = jnp.cumsum(onehot, axis=0) - onehot
-    slot_ids = jnp.sum(before * onehot, axis=1)
-    target = flat_ids * capacity + slot_ids
-    token_rows = jnp.arange(tok_rows * top_count, dtype=jnp.int32) // top_count + 1
-    sources = jnp.zeros((experts * capacity,), jnp.int32).at[target].set(token_rows)
-    padded = jnp.concatenate([jnp.zeros((1, channels), jnp.bfloat16), normed], axis=0)
-    outgoing = padded[sources].reshape(seq_count, local_experts, capacity, channels)
-    worker = functools.partial(expert_work, gate_up=gate_up, down_weight=down_weight)
-    returned = worker(lax.all_to_all(outgoing, "seq", split_axis=0, concat_axis=0, tiled=True))
-    flat_back = returned.reshape(experts * capacity, channels)
-    picked = flat_back[target].reshape(tok_rows, top_count, channels).astype(jnp.float32)
-    combined = jnp.zeros((tok_rows, channels), jnp.float32)
-    for pick_k in range(top_count):
-        combined = combined + gate_weights[:, pick_k : pick_k + 1] * picked[:, pick_k]
-    return (resid_float + combined).astype(jnp.bfloat16)
+    split = jnp.transpose(gate_up, (0, 2, 1, 3))
+    return experts(normed, residual, expert_ids, gate_weights, split, down_weight)
 
 
 def solution(mesh):

time: 275 us -> 163 us (0.59)
  waiting for transfers between devices: 128 us -> 9.51 us
  Pallas kernels: 0 us -> 89 us
  local copies, waits for them, and re-layouts: 30.2 us -> 10.2 us
  blocking collectives: 29.1 us -> 14.1 us
  starting transfers between devices: 37.4 us -> 23.5 us
  between operations: 13.8 us -> 0.3 us
  matrix products: 22.9 us -> 13.1 us
  other arithmetic: 11.2 us -> 2.98 us
    pallas_call x0 -> x1, Pallas kernels: none -> 89 us  [experts(): pl.pallas_call(experts_kernel, out_shape=jax.ShapeDtypeStruct((tokens, wi...]
    psum x1 -> x0, waiting for transfers between devices: 84.8 us -> none  [expert_work(): totals = lax.psum(partials.astype(jnp.bfloat16), 'exp').astype(jnp.float32)]
    all_to_all x2 -> x0, waiting for transfers between devices: 32.9 us -> none  [the longest x1 27.7 us: expert_work(): lax.all_to_all(outgoing, 'seq', split_axis=0, concat_axis=0, tiled=True)]
    all_to_all x1, blocking collectives: 29.1 us -> 14.1 us  [local(): lax.all_to_all(result_long.astype(jnp.bfloat16), 'seq', split_axis=0, con...]
    all_to_all x2 -> x0, starting transfers between devices: 14.9 us -> none  [the longest x1 9.7 us: expert_work(): lax.all_to_all(outgoing, 'seq', split_axis=0, concat_axis=0, tiled=True)]
    gather x2 -> x0, local copies, waits for them, and re-layouts: 9.77 us -> none  [the longest x1 5.05 us: local(): padded[sources].reshape(seq_count, local_experts, capacity, channels)]
    dot_general x2 -> x0, matrix products: 9.74 us -> none  [the longest x1 7.6 us: expert_work(): jnp.einsum('spnc,pcgf->spngf', received, gate_up, preferred_element_type=...]
    slice x2 -> x0, local copies, waits for them, and re-layouts: 7.13 us -> none  [the longest x1 6.85 us: local(): combined = combined + gate_weights[:, pick_k:pick_k + 1] * picked[:, pick_k]]
  transfers between devices with their start and end apart: 6 -> 3, of which waited for: 5 -> 1; matrix products, arithmetic and copies ran while one was open for 3% -> 5% of each run, Pallas kernels for 0% -> 0%
where the time goes in v1:
time: 163 us
  Pallas kernels  89 us (55%)
  starting transfers between devices  23.5 us (14%)
  blocking collectives  14.1 us (9%)
  matrix products  13.1 us (8%)
  local copies, waits for them, and re-layouts  10.2 us (6%)
  waiting for transfers between devices  9.51 us (6%)
  other arithmetic  2.98 us (2%)
    pallas_call x1, Pallas kernels, experts(): pl.pallas_call(experts_kernel, out_shape=jax.ShapeDtypeStruct((tokens, wi...  89 us
    all_to_all x1, blocking collectives, local(): lax.all_to_all(result_long.astype(jnp.bfloat16), 'seq', split_axis=0, con...  14.1 us
    dot_general x12, matrix products, precise(): return jnp.einsum(formula, matrix, operand, precision=lax.Precision.HIGHEST)  13.1 us
    all_to_all x1, starting transfers between devices, local(): lax.all_to_all(paired.astype(jnp.bfloat16), 'seq', split_axis=2, concat_a...  11.4 us
    all_to_all x1, waiting for transfers between devices, local(): lax.all_to_all(paired.astype(jnp.bfloat16), 'seq', split_axis=2, concat_a...  9.5 us
    all_to_all x1, starting transfers between devices, copy_for_each(): return lax.all_to_all(copies, axis, split_axis=0, concat_axis=0, tiled=True)  8.57 us
    unnamed x18, local copies, waits for them, and re-layouts  6.9 us
    ppermute x1, starting transfers between devices, shifted(): return lax.ppermute(value, axis, pairs)  3.54 us
  transfers between devices with their start and end apart: 3, of which 1 were waited for; matrix products, arithmetic and copies ran while one was open for 5% of the time, Pallas kernels for 0%

profile of v1, /device:TPU:5, one launch (start us, length us, event | category | flops | bytes accessed | tf_op | source)
XLA Modules:
  0.0 162.7 jit_solution(12817894069797812276)
XLA Ops:
  0.0 0.7 slice.47
  0.8 3.5 %collective-permute-start = (bf16[3,2,512]{2,1,0:T(2,128)(2,1)S(1)}, bf16[3,2,512]{2,1,0:T(2,128)(2,1)S(1)}, u32[]{:S(2)}, u32[]{:S(2)}) collective-permute-start(bf16[3,2,512]{2,1,0:T(2,128)(2,1)S(1)} %slice.47), channel_id=1, source_target_pairs={{0,8},{8,16},{16,24},{24,32},{32,40},{40,48},{48,56},{56,64},{64,7... | collective-permute-start | bytes 18440 | tf_op jit(solution)/shard_map/ppermute | solution.py:16
  4.3 0.9 fusion.139
  5.2 1.0 convert_bitcast_fusion
  6.2 0.0 collective-permute-done
  6.2 1.1 maximum_convert_fusion
  7.3 0.2 fusion.11
  7.6 0.9 copy.63
  8.5 11.4 %all-to-all-start = ((bf16[2,128,512]{1,0,2:T(2,128)(2,1)}), bf16[2,128,512]{1,0,2:T(2,128)(2,1)S(1)}, u32[]{:S(2)}, u32[]{:S(2)}) async-start(bf16[2,128,512]{1,0,2:T(2,128)(2,1)} %copy.63), calls=%async_computation | async-start | bytes 524288 | tf_op jit(solution)/shard_map/all_to_all | solution.py:453
  19.9 0.1 fusion.76
  20.0 9.5 %all-to-all-done = bf16[2,128,512]{1,0,2:T(2,128)(2,1)S(1)} async-done(((bf16[2,128,512]{1,0,2:T(2,128)(2,1)}), bf16[2,128,512]{1,0,2:T(2,128)(2,1)S(1)}, u32[]{:S(2)}, u32[]{:S(2)}) %all-to-all-start) | async-done | bytes 262176 | tf_op jit(solution)/shard_map/all_to_all | solution.py:453
  29.5 0.7 convolution_bitcast_fusion
  30.2 0.9 multiply_add_fusion
  31.2 1.7 %fusion.9 = f32[2,64,16,128]{3,2,1,0:T(8,128)S(1)} fusion(f32[2,64,128,16]{2,1,3,0:T(8,128)S(1)} %get-tuple-element.7), kind=kOutput, calls=%fused_computation.19 | convolution fusion | flops 402882560 | bytes 2097152 | tf_op jit(solution)/shard_map/qm,akmc->akqc/dot_general | solution.py:35
  32.9 1.7 %fusion.5 = f32[2,64,16,128]{3,2,1,0:T(8,128)S(1)} fusion(f32[2,64,128,16]{2,1,3,0:T(8,128)S(1)} %get-tuple-element.8), kind=kOutput, calls=%fused_computation.15 | convolution fusion | flops 402882560 | bytes 2097152 | tf_op jit(solution)/shard_map/qm,akmc->akqc/dot_general | solution.py:35
  34.6 1.7 %fusion.1 = f32[2,64,128,16]{2,3,1,0:T(8,128)S(1)} fusion(f32[2,64,16,128]{3,2,1,0:T(8,128)S(1)} %fusion.9, f32[2,64,128,16]{2,1,3,0:T(8,128)S(1)} %get-tuple-element.8), kind=kOutput, calls=%fused_computation.4 | convolution fusion | flops 403144704 | bytes 3145728 | tf_op jit(solution)/shard_map/qm,akmc->akqc/dot_general | solution.py:35
  36.3 1.7 %fusion = f32[2,64,128,16]{2,3,1,0:T(8,128)S(1)} fusion(f32[2,64,16,128]{3,2,1,0:T(8,128)S(1)} %fusion.5, f32[2,64,128,16]{2,1,3,0:T(8,128)S(1)} %get-tuple-element.7), kind=kOutput, calls=%fused_computation.2 | convolution fusion | flops 403144704 | bytes 3145728 | tf_op jit(solution)/shard_map/qm,akmc->akqc/dot_general | solution.py:35
  38.1 0.0 copy-start.1
  38.1 0.0 copy-start.4
  38.1 0.1 multiply_subtract_fusion.1
  38.2 0.0 copy-start.2
  38.2 0.0 copy-start.3
  38.2 0.8 fusion.17
  39.1 0.8 fusion.13
  39.9 0.8 convolution_add_fusion.1
  40.7 1.1 add_bitcast_fusion
  41.8 0.6 fusion.20
  42.4 0.6 fusion.4
  42.9 0.1 copy.72
  43.0 14.1 %all_to_all.31 = bf16[32,128,16]{1,2,0:T(8,128)(2,1)S(1)} all-to-all(bf16[32,128,16]{1,2,0:T(8,128)(2,1)S(1)} %copy.72), channel_id=1, replica_groups=mesh['seq'=32,'exp'=8] {'seq'}, dimensions={0} | all-to-all | bytes 262144 | tf_op jit(solution)/shard_map/all_to_all | solution.py:457
  57.2 0.1 copy.73
  57.3 0.0 copy-done.1
  57.3 0.0 copy-done.4
  57.3 0.2 fusion.22
  57.5 0.6 broadcast_in_dim.2
  58.1 8.6 %all-to-all-start.2 = ((f32[8,1,128]{2,1,0:T(1,128)}), f32[8,1,128]{2,1,0:T(1,128)S(1)}, u32[]{:S(2)}, u32[]{:S(2)}) async-start(f32[8,1,128]{2,1,0:T(1,128)} %broadcast_in_dim.2), calls=%async_computation.2 | async-start | bytes 8192 | tf_op jit(solution)/shard_map/all_to_all | solution.py:21
  66.7 0.0 copy-done.2
  66.7 0.1 copy.76.ids
  66.8 0.0 copy-done.3
  66.8 0.1 copy.77.weights
  66.9 0.0 copy-start
  66.9 6.0 %copy.113 = bf16[2,512,2,1408]{3,1,2,0:T(8,128)(2,1)} copy(bf16[2,512,2,1408]{3,2,1,0:T(2,128)(2,1)} %param.16) | data formatting | bytes 11534336 | tf_op args[6]
  72.9 0.0 all-to-all-done.2
  72.9 0.0 copy-done.5
  72.9 0.1 fusion.24.normed
  73.0 0.0 copy-done
  73.0 89.0 %experts.1 = bf16[128,512]{1,0:T(8,128)(2,1)S(1)} custom-call(bf16[128,512]{1,0:T(8,128)(2,1)S(1)} %fusion.24.normed, bf16[128,512]{1,0:T(8,128)(2,1)S(1)} %get-tuple-element.6.resid, s32[128,6]{1,0:T(8,128)S(1)} %copy.76.ids, f32[128,6]{1,0:T(8,128)S(1)} %copy.77.weights, bf16[2,2,512,1408]{3,2,1,0:T(8,128)(2,1)} %bitcast.108, bf16[2,1408,512]{2,1,0:T(8,128)(2,1)S(1)} %copy-done), custom_call_target="tpu_custom_call" | custom-call | tf_op jit(solution)/shard_map/experts/pallas_call | solution.py:380
  162.0 0.7 copy.116
  (8 shorter events, 0.1 us)
Async XLA Ops:
  0.8 5.4 %collective-permute-start = (bf16[3,2,512]{2,1,0:T(2,128)(2,1)S(1)}, bf16[3,2,512]{2,1,0:T(2,128)(2,1)S(1)}, u32[]{:S(2)}, u32[]{:S(2)}) collective-permute-start(bf16[3,2,512]{2,1,0:T(2,128)(2,1)S(1)} %slice.47), channel_id=1, source_target_pairs={{0,8},{8,16},{16,24},{24,32},{32,40},{40,48},{48,56},{56,64},{64,7... | collective-permute-start | bytes 18440 | tf_op jit(solution)/shard_map/ppermute | solution.py:16
  8.5 21.0 %all-to-all-start = ((bf16[2,128,512]{1,0,2:T(2,128)(2,1)}), bf16[2,128,512]{1,0,2:T(2,128)(2,1)S(1)}, u32[]{:S(2)}, u32[]{:S(2)}) async-start(bf16[2,128,512]{1,0,2:T(2,128)(2,1)} %copy.63), calls=%async_computation | async-start | bytes 524288 | tf_op jit(solution)/shard_map/all_to_all | solution.py:453
  38.1 19.3 %copy-start.1 = (bf16[128,512]{1,0:T(8,128)(2,1)S(1)}, bf16[128,512]{1,0:T(8,128)(2,1)}, u32[]{:S(2)}) copy-start(bf16[128,512]{1,0:T(8,128)(2,1)} %param.11) | copy-start | bytes 393220
  38.1 19.3 %copy-start.4 = (f32[512]{0:T(512)S(1)}, f32[512]{0:T(512)}, u32[]{:S(2)}) copy-start(f32[512]{0:T(512)} %param.14) | copy-start | bytes 6148
  38.2 28.4 %copy-start.2 = (s32[128,6]{0,1:T(8,128)S(1)}, s32[128,6]{0,1:T(8,128)}, u32[]{:S(2)}) copy-start(s32[128,6]{0,1:T(8,128)} %param.18) | copy-start | bytes 9220
  38.2 28.5 %copy-start.3 = (f32[128,6]{0,1:T(8,128)S(1)}, f32[128,6]{0,1:T(8,128)}, u32[]{:S(2)}) copy-start(f32[128,6]{0,1:T(8,128)} %param.19) | copy-start | bytes 9220
  58.1 14.8 %all-to-all-start.2 = ((f32[8,1,128]{2,1,0:T(1,128)}), f32[8,1,128]{2,1,0:T(1,128)S(1)}, u32[]{:S(2)}, u32[]{:S(2)}) async-start(f32[8,1,128]{2,1,0:T(1,128)} %broadcast_in_dim.2), calls=%async_computation.2 | async-start | bytes 8192 | tf_op jit(solution)/shard_map/all_to_all | solution.py:21
  66.9 6.0 %copy-start.5 = (f32[512]{0:T(512)S(1)}, f32[512]{0:T(512)}, u32[]{:S(2)}) copy-start(f32[512]{0:T(512)} %param.15) | copy-start | bytes 6148
  66.9 6.1 %copy-start = (bf16[2,1408,512]{2,1,0:T(8,128)(2,1)S(1)}, bf16[2,1408,512]{2,1,0:T(8,128)(2,1)}, u32[]{:S(2)}) copy-start(bf16[2,1408,512]{2,1,0:T(8,128)(2,1)} %down.1) | copy-start | bytes 8650756
